TPU v7x, 32 devices: a whole 2x2x4 slice. The times are simulated.
32 devices in a mesh: lat: 8 (over z, y), fld: 4 (over x, core).
Axes of the slice: x: 2, y: 2, z: 4, core: 2. Of those that a mesh axis runs over, the one named last changes fastest.
Arguments:
- grid_fields: bfloat16 [96, 1280, 2560], P('fld', 'lat'), may hold values from -6 to 6
- assign: int32 [320], replicated, may hold values from 0 to 319, each once
- limits: int32 [3], replicated, may hold values from 60 to 319, as said below
- legendre: bfloat16 [320, 641, 640], P('lat', None, 'fld'), may hold values from -0.25 to 0.25
- synth_one: bfloat16 [320, 320, 320], P('lat'), may hold values from -0.3125 to 0.3125
- synth_two: bfloat16 [320, 160, 160], P('lat'), may hold values from -0.5 to 0.5
- synth_three: bfloat16 [320, 80, 80], P('lat'), may hold values from -0.625 to 0.625
Outputs:
- spectrum: bfloat16 [96, 2, 320, 641], P('fld', None, 'lat')
- grid_one: float32 [96, 640, 1280], P('fld', 'lat')
- grid_two: float32 [96, 320, 640], P('fld', 'lat')
- grid_three: float32 [96, 160, 320], P('fld', 'lat')
Inputs may be any that keep to these rules, and one draw needn't show every extreme that they name: assign is a permutation; slot q stands for the wavenumbers assign[q] and 639 - assign[q]. limits[0] is 319, limits[2] is 60, and limits[1] lies between 120 and 159.
All inputs are finite; a program needn't handle non-finite values.
Results may differ from a plain program's by a relative error of at most 0.0077.
Values may be sent and summed in bfloat16 or wider, within the bound.
A program may use at most 256 MiB of HBM per device.

v0:
```python
import math

import jax
import jax.numpy as jnp
from jax import lax
from jax.sharding import PartitionSpec as P


CHUNKS = 1


def choose_pair(values, limit_of):
    ranks = jnp.arange(values.shape[-1], dtype=jnp.int32)
    keep_mask = ranks[None, :] < limit_of[:, None]
    return jnp.where(keep_mask[None, None], values[:, :, :, 0], values[:, :, :, 1])


def select_rows(sym_prod, anti_prod, own_pairs, wave_total):
    first_rows = choose_pair(sym_prod, (wave_total + 1 - own_pairs) // 2)
    later_rows = choose_pair(anti_prod, (wave_total - own_pairs) // 2)
    return jnp.concatenate([first_rows, later_rows], axis=3)


def level_rows_of(spectrum, own_pairs, limit, synth_table, lat_count):
    half_rows = synth_table.shape[1] // 2
    sym_rows = spectrum.shape[3] // 2 + 1
    step_rows = 2 * jnp.arange(half_rows, dtype=jnp.int32)
    keep_sym = own_pairs[:, None] + step_rows[None, :] <= limit
    keep_anti = own_pairs[:, None] + 1 + step_rows[None, :] <= limit
    zero_value = jnp.zeros((), jnp.bfloat16)
    kept_sym = jnp.where(keep_sym[None, None], spectrum[..., :half_rows], zero_value)
    kept_anti = jnp.where(
        keep_anti[None, None], spectrum[..., sym_rows : sym_rows + half_rows], zero_value
    )
    even_part = jnp.einsum(
        "fcqk,qkj->qcfj", kept_sym, synth_table[:, :half_rows], preferred_element_type=jnp.float32
    )
    odd_part = jnp.einsum(
        "fcqk,qkj->qcfj", kept_anti, synth_table[:, half_rows:], preferred_element_type=jnp.float32
    )
    north = (even_part + odd_part).astype(jnp.bfloat16)
    south = jnp.flip((even_part - odd_part).astype(jnp.bfloat16), axis=3)
    slots, parts, fields, half_lat = north.shape
    owners = lat_count // 2
    halves = [
        part.reshape(slots * parts, fields, owners, half_lat // owners)
        .transpose(2, 0, 1, 3)
        .reshape(owners, slots * parts, -1)
        for part in (north, south)
    ]
    return jnp.concatenate(halves, axis=0)


def quarter_of(values, axis):
    return lax.broadcasted_iota(jnp.int32, values.shape, axis).reshape(-1)


def turned_cosine(waves, quarters, places):
    length = places.shape[0]
    turn_count = (waves[:, None] * places[None, :] + quarters[:, None] * (length // 4)) % length
    return jnp.cos(turn_count.astype(jnp.float32) * (2.0 * math.pi / length))


def inverse_table(order, lon_length):
    waves = jnp.stack([order, order], axis=1)
    weight = jnp.where(waves == 0, 1.0, 2.0).astype(jnp.float32) / math.sqrt(lon_length)
    places = jnp.arange(lon_length, dtype=jnp.int32)
    table = turned_cosine(waves.reshape(-1), quarter_of(waves, 1), places)
    return (table * weight.reshape(-1)[:, None]).astype(jnp.bfloat16)


def on_device(grid_fields, assign, limits, legendre, synth_one, synth_two, synth_three):
    lat_count = lax.axis_size("lat")
    field_count, row_count, lon_total = grid_fields.shape
    pair_total = assign.shape[0]
    pair_local = pair_total // lat_count
    wave_total = 2 * pair_total
    sym_rows = pair_total + 1
    chunks = CHUNKS
    while pair_local % chunks:
        chunks -= 1
    slots = pair_local // chunks
    half_count = lat_count // 2
    synth_tables = (synth_one, synth_two, synth_three)
    dft_scale = 1.0 / math.sqrt(lon_total)
    flat_grid = grid_fields.reshape(field_count * row_count, lon_total)
    by_owner = assign.reshape(lat_count, chunks, slots)
    own_all = lax.dynamic_index_in_dim(by_owner, lax.axis_index("lat"), 0, keepdims=False)

    places = jnp.arange(lon_total, dtype=jnp.int32)
    sent_rows = []
    gathered = []
    for at in range(chunks):
        own_block = legendre[at * slots : (at + 1) * slots]
        gathered.append(
            [
                lax.all_gather(part, "fld", axis=2, tiled=True)
                for part in (own_block[:, :sym_rows], own_block[:, sym_rows:])
            ]
        )
    for at in range(chunks):
        waves = jnp.stack([by_owner[:, at], wave_total - 1 - by_owner[:, at]], axis=2)
        waves = jnp.stack([waves, waves], axis=1)
        dft_table = (
            turned_cosine(waves.reshape(-1), quarter_of(waves, 1), places) * dft_scale
        ).astype(jnp.bfloat16)
        fourier = lax.dot_general(
            dft_table,
            flat_grid,
            (((1,), (1,)), ((), ())),
            preferred_element_type=jnp.float32,
        ).astype(jnp.bfloat16)
        sent_rows.append(
            lax.all_to_all(
                fourier.reshape(lat_count, 4 * slots, field_count * row_count),
                "lat",
                split_axis=0,
                concat_axis=0,
                tiled=True,
            )
        )

    spectra = []
    arrived = []
    for at in range(chunks):
        own_pairs = own_all[at]
        split_six = (
            sent_rows[at]
            .reshape(lat_count, 2, slots, 2, field_count, row_count)
            .transpose(2, 1, 3, 4, 0, 5)
        )
        flat_shape = (slots, 2, 2, field_count, half_count * row_count)
        split_six = lax.optimization_barrier(split_six)
        north_rows = split_six[..., :half_count, :].reshape(flat_shape).astype(jnp.float32)
        south_rows = jnp.flip(split_six[..., half_count:, :].reshape(flat_shape), axis=4).astype(
            jnp.float32
        )
        symmetric = (north_rows + south_rows).astype(jnp.bfloat16)
        antisym = (north_rows - south_rows).astype(jnp.bfloat16)
        block_piece = gathered[at]
        sym_add = jnp.einsum(
            "scwkj,srj->kcswr",
            symmetric,
            block_piece[0],
            preferred_element_type=jnp.float32,
        )
        anti_add = jnp.einsum(
            "scwkj,srj->kcswr",
            antisym,
            block_piece[1],
            preferred_element_type=jnp.float32,
        )
        spectrum = select_rows(sym_add, anti_add, own_pairs, wave_total).astype(jnp.bfloat16)
        spectra.append(spectrum)
        level_blocks = [
            level_rows_of(
                spectrum,
                own_pairs,
                limits[level],
                synth_tables[level][at * slots : (at + 1) * slots],
                lat_count,
            )
            for level in range(3)
        ]
        arrived.append(
            lax.all_to_all(
                jnp.concatenate(level_blocks, axis=2),
                "lat",
                split_axis=0,
                concat_axis=0,
                tiled=True,
            )
        )

    order = by_owner.transpose(1, 0, 2).reshape(-1)
    all_rows = jnp.stack(arrived, axis=0).reshape(2 * pair_total, -1)
    grids_out = []
    start = 0
    for level in range(3):
        level_lat = 2 * synth_tables[level].shape[1]
        own_rows = level_lat // lat_count
        width = field_count * own_rows
        inverse = inverse_table(order, 2 * level_lat)
        grids_out.append(
            lax.dot_general(
                all_rows[:, start : start + width],
                inverse,
                (((0,), (0,)), ((), ())),
                preferred_element_type=jnp.float32,
            ).reshape(field_count, own_rows, -1)
        )
        start += width
    return (jnp.concatenate(spectra, axis=2), grids_out[0], grids_out[1], grids_out[2])


def solution(mesh):
    return jax.shard_map(
        on_device,
        mesh=mesh,
        in_specs=(
            P("fld", "lat", None),
            P(),
            P(),
            P("lat", None, "fld"),
            P("lat", None, None),
            P("lat", None, None),
            P("lat", None, None),
        ),
        out_specs=(
            P("fld", None, "lat", None),
            P("fld", "lat", None),
            P("fld", "lat", None),
            P("fld", "lat", None),
        ),
        check_vma=False,
    )
```

profile of v0, /device:TPU:0, one launch (start us, length us, event | category | flops | bytes accessed | tf_op | source)
XLA Modules:
  0.0 707.5 jit_solution(14144387731433710482)
XLA Ops:
  7.2 8.0 %slice.89 = bf16[40,320,160]{1,2,0:T(8,128)(2,1)} slice(bf16[40,641,160]{1,2,0:T(8,128)(2,1)} %param.10), slice={[0:40], [321:641], [0:160]} | slice | bytes 8192000 | tf_op jit(solution)/shard_map/slice | solution.py:98
  15.3 5.1 slice.86
  21.8 52.7 %fusion.157 = bf16[1280,2560]{1,0:T(8,128)(2,1)S(1)} fusion(s32[1280]{0:T(1024)S(1)} %mul.206, s32[1280]{0:T(1024)S(1)} %mul.200), kind=kLoop, calls=%fused_computation.11.clone.clone.1 | loop fusion | flops 39321600 | bytes 6563840 | tf_op jit(solution)/shard_map/dot_general | solution.py:107
  74.5 30.7 %convolution_convert_fusion = bf16[1280,3840]{1,0:T(8,128)(2,1)} fusion(bf16[3840,2560]{1,0:T(8,128)(2,1)} %bitcast.157, bf16[1280,2560]{1,0:T(8,128)(2,1)S(1)} %fusion.157), kind=kOutput, calls=%fused_computation.6 | convolution fusion | flops 25170739200 | bytes 36044800 | tf_op jit(solution)/shard_map/dot_general | solution.py:107
  105.2 7.5 %all-to-all-start = ((bf16[8,160,3840]{2,1,0:T(8,128)(2,1)}), bf16[8,160,3840]{2,1,0:T(8,128)(2,1)}, u32[]{:S(2)}, u32[]{:S(2)}) async-start(bf16[8,160,3840]{2,1,0:T(8,128)(2,1)} %bitcast.144), calls=%async_computation | async-start | bytes 19660800 | tf_op jit(solution)/shard_map/all_to_all | solution.py:114
  115.8 210.9 %all-to-all-done = bf16[8,160,3840]{2,1,0:T(8,128)(2,1)} async-done(((bf16[8,160,3840]{2,1,0:T(8,128)(2,1)}), bf16[8,160,3840]{2,1,0:T(8,128)(2,1)}, u32[]{:S(2)}, u32[]{:S(2)}) %all-to-all-start) | async-done | bytes 9830432 | tf_op jit(solution)/shard_map/all_to_all | solution.py:114
  326.7 26.7 %reshape.405 = bf16[8,2,40,2,24,160]{5,4,3,2,1,0:T(8,128)(2,1)} reshape(bf16[8,160,3840]{2,1,0:T(8,128)(2,1)} %all-to-all-done) | data formatting | bytes 19660800 | tf_op jit(solution)/shard_map/reshape | solution.py:129
  353.4 15.4 %copy.53 = bf16[8,2,40,2,24,160]{5,0,4,3,1,2:T(8,128)(2,1)S(1)} copy(bf16[8,2,40,2,24,160]{5,4,3,2,1,0:T(8,128)(2,1)} %reshape.405) | data formatting | bytes 19660800 | tf_op jit(solution)/shard_map/reshape | solution.py:129
  368.7 10.2 %fusion.143 = (bf16[40,2,2,24,4,160]{5,4,3,2,1,0:T(4,128)(2,1)}, f32[40,2,2,24,4,160]{5,4,3,2,1,0:T(4,128)}) fusion(bf16[40,2,2,24,8,160]{5,4,3,2,1,0:T(8,128)(2,1)S(1)} %bitcast.143), kind=kLoop, calls=%fused_computation.198 | loop fusion | flops 2457600 | bytes 24576000 | tf_op jit(solution)/shard_map/slice | solution.py:135
  378.9 16.6 %reshape.422 = f32[40,2,2,24,640]{4,3,2,1,0:T(8,128)} reshape(f32[40,2,2,24,4,160]{5,4,3,2,1,0:T(4,128)} %get-tuple-element.17) | data formatting | bytes 19660800 | tf_op jit(solution)/shard_map/convert_element_type | solution.py:134
  395.5 11.8 %reshape.406 = bf16[40,2,2,24,640]{4,3,2,1,0:T(8,128)(2,1)} reshape(bf16[40,2,2,24,4,160]{5,4,3,2,1,0:T(4,128)(2,1)} %get-tuple-element.16) | data formatting | bytes 9830400 | tf_op jit(solution)/shard_map/reshape | solution.py:135
  407.3 13.7 %rev.16 = bf16[40,2,2,24,640]{4,3,2,1,0:T(8,128)(2,1)} reverse(bf16[40,2,2,24,640]{4,3,2,1,0:T(8,128)(2,1)} %reshape.406), dimensions={4} | reverse | bytes 9830400 | tf_op jit(solution)/shard_map/jit(_flip)/rev | solution.py:135
  420.9 12.8 %fusion.46 = bf16[24,2,40,2,320]{4,0,1,2,3:T(8,128)(2,1)S(1)} fusion(bf16[40,320,640]{1,2,0:T(8,128)(2,1)} %all-gather.5.cloned.1.call-done, f32[40,2,2,24,640]{4,3,2,1,0:T(8,128)} %reshape.422, bf16[40,2,2,24,640]{4,3,2,1,0:T(8,128)(2,1)} %rev.16), kind=kOutput, calls=%fused_computation.56 | convolution fusion | flops 1580236800 | bytes 33587200 | tf_op jit(solution)/shard_map/scwkj,srj->kcswr/dot_general | solution.py:147
  438.0 5.1 fusion.22
  443.1 13.2 %fusion.41 = bf16[24,2,40,2,321]{4,0,3,1,2:T(8,128)(2,1)S(1)} fusion(bf16[40,321,640]{1,2,0:T(8,128)(2,1)} %all-gather.3.cloned.1.call-done, f32[40,2,2,24,640]{4,3,2,1,0:T(8,128)} %reshape.422, bf16[40,2,2,24,640]{4,3,2,1,0:T(8,128)(2,1)} %rev.16), kind=kOutput, calls=%fused_computation.55 | convolution fusion | flops 1585152000 | bytes 33646080 | tf_op jit(solution)/shard_map/scwkj,srj->kcswr/dot_general | solution.py:141
  464.6 4.2 copy.27
  486.9 4.5 reshape.413
  491.4 4.1 copy.23
  497.6 4.5 reshape.411
  502.1 4.0 copy.22
  508.3 6.1 fusion.74
  514.4 4.9 reverse
  522.5 4.8 reshape.409
  530.4 4.2 reshape.410
  534.6 4.8 reshape.407
  542.6 4.2 reshape.408
  552.9 7.5 %concatenate.20 = bf16[8,80,3360]{2,1,0:T(8,128)(2,1)} concatenate(bf16[8,80,1920]{2,1,0:T(8,128)(2,1)} %pad_maximum_fusion.1, bf16[8,80,960]{2,1,0:T(8,128)(2,1)} %pad_maximum_fusion.2, bf16[8,80,480]{2,1,0:T(8,128)(2,1)} %pad_maximum_fusion.3), dimensions={2} | concatenate | bytes 8601600 | tf_op jit(solution)/shard_map/concatenate | solution.py:167
  560.4 4.8 all-to-all-start.1
  569.7 92.8 %all-to-all-done.1 = bf16[8,80,3360]{2,1,0:T(8,128)(2,1)} async-done(((bf16[8,80,3360]{2,1,0:T(8,128)(2,1)}), bf16[8,80,3360]{2,1,0:T(8,128)(2,1)}, u32[]{:S(2)}, u32[]{:S(2)}) %all-to-all-start.1) | async-done | bytes 4300832 | tf_op jit(solution)/shard_map/all_to_all | solution.py:166
  662.5 5.6 fusion.97
  669.2 20.9 %fusion.51 = f32[1920,1280]{1,0:T(8,128)} fusion(bf16[640,3360]{1,0:T(8,128)(2,1)} %bitcast.46, f32[640]{0:T(1024)S(1)} %get-tuple-element.25, s32[640]{0:T(1024)S(1)} %mul.222, s32[640]{0:T(1024)S(1)} %mul.216), kind=kOutput, calls=%fused_computation.57 | convolution fusion | flops 3155558400 | bytes 12295680 | tf_op jit(solution)/shard_map/dot_general | solution.py:185
  690.0 10.2 %fusion.76 = f32[960,640]{1,0:T(8,128)} fusion(bf16[640,3360]{1,0:T(8,128)(2,1)} %bitcast.46, f32[640]{0:T(1024)S(1)} %get-tuple-element.24, s32[640]{0:T(1024)S(1)} %mul.232, s32[640]{0:T(1024)S(1)} %mul.216), kind=kOutput, calls=%fused_computation.89 | convolution fusion | flops 791347200 | bytes 3776000 | tf_op jit(solution)/shard_map/dot_general | solution.py:185
  (81 shorter events, 60.6 us)
Async XLA Ops:
  7.2 413.8 %all-gather.5.cloned.1.call-start = ((), (), s32[]{:S(2)}) async-start(), calls=%async_computation.3 | async-start | bytes 24576000 | tf_op jit(solution)/shard_map/all_gather | solution.py:97
  15.2 427.9 %all-gather.3.cloned.1.call-start = ((), (), s32[]{:S(2)}) async-start(), calls=%async_computation.2 | async-start | bytes 24576000 | tf_op jit(solution)/shard_map/all_gather | solution.py:97
  20.4 0.7 copy-start.7
  105.2 7.6 %copy-start.8 = (s32[3]{0:T(128)S(1)}, s32[3]{0:T(128)}, u32[]{:S(2)}) copy-start(s32[3]{0:T(128)} %param.9) | copy-start | bytes 40
  105.2 221.5 %all-to-all-start = ((bf16[8,160,3840]{2,1,0:T(8,128)(2,1)}), bf16[8,160,3840]{2,1,0:T(8,128)(2,1)}, u32[]{:S(2)}, u32[]{:S(2)}) async-start(bf16[8,160,3840]{2,1,0:T(8,128)(2,1)} %bitcast.144), calls=%async_computation | async-start | bytes 19660800 | tf_op jit(solution)/shard_map/all_to_all | solution.py:114
  433.7 1.1 copy-start.5
  433.7 2.5 copy-start.3
  456.3 1.2 copy-start.2
  456.3 1.4 copy-start.6
  539.4 7.3 %copy-start.4 = (bf16[4,80,480]{2,1,0:T(8,128)(2,1)S(1)}, bf16[4,80,480]{2,1,0:T(8,128)(2,1)}, u32[]{:S(2)}) copy-start(bf16[4,80,480]{2,1,0:T(8,128)(2,1)} %copy.29) | copy-start | bytes 921604
  546.7 4.5 copy-start
  546.7 4.5 copy-start.1
  560.4 102.0 %all-to-all-start.1 = ((bf16[8,80,3360]{2,1,0:T(8,128)(2,1)}), bf16[8,80,3360]{2,1,0:T(8,128)(2,1)}, u32[]{:S(2)}, u32[]{:S(2)}) async-start(bf16[8,80,3360]{2,1,0:T(8,128)(2,1)} %concatenate.20), calls=%async_computation.1 | async-start | bytes 8847360 | tf_op jit(solution)/shard_map/all_to_all | solution.py:166
Sparse Core Ops, SparseCore 0:
  15.4 127.1 all-gather.4
  144.1 124.3 all-gather.2
where the time goes:
time: 718 us; the launch traced here: 708 us
  waiting for transfers between devices  304 us (42%)
  local copies, waits for them, and re-layouts  191 us (27%)
  matrix products  113 us (16%)
  other arithmetic  73 us (10%)
  between operations  14.8 us (2%)
  starting transfers between devices  12.3 us (2%)
    all_to_all x1, waiting for transfers between devices, on_device(): lax.all_to_all(fourier.reshape(lat_count, 4 * slots, field_count * row_co...  211 us
    all_to_all x1, waiting for transfers between devices, on_device(): lax.all_to_all(jnp.concatenate(level_blocks, axis=2), 'lat', split_axis=0...  92.8 us
    dot_general x1, other arithmetic, on_device(): lax.dot_general(dft_table, flat_grid, (((1,), (1,)), ((), ())), preferred...  52.7 us
    reshape x2, local copies, waits for them, and re-layouts, on_device(): split_six = sent_rows[at].reshape(lat_count, 2, slots, 2, field_count, ro...  42.1 us
    dot_general x3, matrix products, on_device(): lax.dot_general(all_rows[:, start:start + width], inverse, (((0,), (0,)),...  36.7 us
    dot_general x1, matrix products, on_device(): lax.dot_general(dft_table, flat_grid, (((1,), (1,)), ((), ())), preferred...  30.7 us
    reshape x8, local copies, waits for them, and re-layouts, level_rows_of(): part.reshape(slots * parts, fields, owners, half_lat // owners)  30.3 us
    unnamed x24, local copies, waits for them, and re-layouts  20.6 us
  transfers between devices with their start and end apart: 4, of which 2 were waited for; matrix products, arithmetic and copies ran while one was open for 30% of the time, Pallas kernels for 0%

commit v1 on v0

--- a/solution.py
+++ b/solution.py
@@ -1,8 +1,11 @@
+import functools
 import math
 
 import jax
 import jax.numpy as jnp
 from jax import lax
+from jax.experimental import pallas as pl
+from jax.experimental.pallas import tpu as pltpu
 from jax.sharding import PartitionSpec as P
 
 
@@ -57,8 +60,26 @@
 
 def turned_cosine(waves, quarters, places):
     length = places.shape[0]
-    turn_count = (waves[:, None] * places[None, :] + quarters[:, None] * (length // 4)) % length
-    return jnp.cos(turn_count.astype(jnp.float32) * (2.0 * math.pi / length))
+    inner = 128 if length % 128 == 0 else math.gcd(length, 128)
+    coarse = jnp.arange(length // inner, dtype=jnp.int32) * inner
+    fine = jnp.arange(inner, dtype=jnp.int32)
+    step = 2.0 * math.pi / length
+
+    def angles(at, shift):
+        return ((waves[:, None] * at[None, :] + shift) % length).astype(jnp.float32) * step
+
+    outer_angle = angles(coarse, quarters[:, None] * (length // 4))
+    inner_angle = angles(fine, 0)
+    outer_cos, outer_sin = jnp.cos(outer_angle), jnp.sin(outer_angle)
+    inner_cos, inner_sin = jnp.cos(inner_angle), jnp.sin(inner_angle)
+    outer_cos, outer_sin, inner_cos, inner_sin = lax.optimization_barrier(
+        (outer_cos, outer_sin, inner_cos, inner_sin)
+    )
+    pieces = [
+        outer_cos[:, at : at + 1] * inner_cos - outer_sin[:, at : at + 1] * inner_sin
+        for at in range(length // inner)
+    ]
+    return jnp.concatenate(pieces, axis=1)
 
 
 def inverse_table(order, lon_length):
@@ -69,7 +90,7 @@
     return (table * weight.reshape(-1)[:, None]).astype(jnp.bfloat16)
 
 
-def on_device(grid_fields, assign, limits, legendre, synth_one, synth_two, synth_three):
+def plain_on_device(grid_fields, assign, limits, legendre, synth_one, synth_two, synth_three):
     lat_count = lax.axis_size("lat")
     field_count, row_count, lon_total = grid_fields.shape
     pair_total = assign.shape[0]
@@ -193,6 +214,638 @@
     return (jnp.concatenate(spectra, axis=2), grids_out[0], grids_out[1], grids_out[2])
 
 
+F32 = jnp.float32
+BF16 = jnp.bfloat16
+LANES = 128
+GROUP = 4
+SLOTS = 8
+VMEM_LIMIT = 56 * 1024 * 1024
+
+
+def fits(grid_fields, assign, limits, legendre, synth_one, synth_two, synth_three):
+    field_count, row_count, lon_total = grid_fields.shape
+    lat_count = lax.axis_size("lat")
+    pair_local = assign.shape[0] // lat_count
+    rest = row_count - LANES
+    counts = (synth_one.shape[1], synth_two.shape[1], synth_three.shape[1])
+    owns = [2 * count // lat_count for count in counts]
+    return (
+        lat_count == 8
+        and lax.axis_size("fld") * row_count == legendre.shape[2] * lax.axis_size("fld")
+        and lax.axis_size("fld") == lat_count // 2
+        and rest * GROUP == LANES
+        and field_count == 6 * GROUP
+        and lon_total % LANES == 0
+        and pair_local % SLOTS == 0
+        and legendre.shape[1] == 2 * assign.shape[0] + 1
+        and (2 * assign.shape[0]) % LANES == 0
+        and owns[0] % 16 == 0
+        and owns[0] + owns[1] + 8 == LANES
+        and 3 * owns[2] <= 64
+        and counts[0] <= 384
+        and counts[1] <= 256
+        and counts[2] <= LANES
+    )
+
+
+def nt_dot(left, right):
+    return lax.dot_general(left, right, (((1,), (1,)), ((), ())), preferred_element_type=F32)
+
+
+def nn_dot(left, right):
+    return jnp.dot(left, right, preferred_element_type=F32)
+
+
+def eye_of(size):
+    rows = lax.broadcasted_iota(jnp.int32, (size, size), 0)
+    columns = lax.broadcasted_iota(jnp.int32, (size, size), 1)
+    return jnp.where(rows == columns, 1.0, 0.0).astype(BF16)
+
+
+def picks(rows, source):
+    return jnp.where(rows == source, 1.0, 0.0).astype(BF16)
+
+
+def dft_body(chunks, scale, shift_ref, ocos, osin, icos, isin, grid_ref, after_ref, *rest):
+    outs, table, stage = rest[:8], rest[8], rest[9]
+    per_slot = 2 * SLOTS
+    side = 8 * per_slot
+    coefs = 2 * side
+    steps = ocos.shape[0]
+
+    @pl.when(pl.program_id(0) == 0)
+    def _():
+        for at in range(chunks):
+            lanes = slice(at * side, (at + 1) * side)
+            cos_in, sin_in = icos[:, lanes] * scale, isin[:, lanes] * scale
+            for step in range(steps):
+                cos_out, sin_out = ocos[step : step + 1, lanes], osin[step : step + 1, lanes]
+                rows = slice(step * LANES, (step + 1) * LANES)
+                table[rows, at * coefs : at * coefs + side] = (
+                    cos_out * cos_in - sin_out * sin_in
+                ).astype(BF16)
+                table[rows, at * coefs + side : (at + 1) * coefs] = (
+                    -(sin_out * cos_in + cos_out * sin_in)
+                ).astype(BF16)
+
+    group, row_count, lon_total = grid_ref.shape
+    small = row_count - LANES
+    values = grid_ref[...].reshape(group * row_count, lon_total)
+    first = pl.multiple_of(shift_ref[0], 16)
+    second = pl.multiple_of(shift_ref[1], 16)
+    eye = eye_of(coefs)
+    for at in range(chunks):
+        stage[...] = nn_dot(values, table[:, at * coefs : (at + 1) * coefs]).astype(BF16)
+        pieces = [stage[pl.ds(f * row_count + first, LANES), :] for f in range(group)]
+        pieces += [stage[pl.ds(f * row_count + second, small), :] for f in range(group)]
+        turned = nt_dot(eye, jnp.concatenate(pieces, axis=0)).astype(BF16)
+        for k in range(8):
+            for c in range(2):
+                start = c * side + k * per_slot
+                for tile in range(group + 1):
+                    outs[k][at, 0, tile, c * per_slot : (c + 1) * per_slot, :] = turned[
+                        start : start + per_slot, tile * LANES : (tile + 1) * LANES
+                    ]
+
+
+def dft_call(shift, trig, grid_fields, after):
+    ocos, osin, icos, isin = trig
+    field_count, row_count, lon_total = grid_fields.shape
+    chunks = ocos.shape[1] // (8 * 2 * SLOTS)
+    coefs = 8 * 4 * SLOTS
+    groups = field_count // GROUP
+    whole = lambda shape: pl.BlockSpec(shape, lambda g, *_: (0,) * len(shape))
+    out = jax.ShapeDtypeStruct((chunks, groups, GROUP + 1, 4 * SLOTS, LANES), BF16)
+    return pl.pallas_call(
+        functools.partial(dft_body, chunks, 1.0 / math.sqrt(lon_total)),
+        grid_spec=pltpu.PrefetchScalarGridSpec(
+            num_scalar_prefetch=1,
+            grid=(groups,),
+            in_specs=[
+                whole(ocos.shape),
+                whole(osin.shape),
+                whole(icos.shape),
+                whole(isin.shape),
+                pl.BlockSpec((GROUP, row_count, lon_total), lambda g, *_: (g, 0, 0)),
+                pl.BlockSpec(memory_space=pl.ANY),
+            ],
+            out_specs=[
+                pl.BlockSpec(
+                    (chunks, 1, GROUP + 1, 4 * SLOTS, LANES), lambda g, *_: (0, g, 0, 0, 0)
+                )
+                for _ in range(8)
+            ],
+            scratch_shapes=[
+                pltpu.VMEM((lon_total, chunks * coefs), BF16),
+                pltpu.VMEM((GROUP * row_count, coefs), BF16),
+            ],
+        ),
+        out_shape=[out] * 8,
+        compiler_params=pltpu.CompilerParams(
+            dimension_semantics=("arbitrary",), vmem_limit_bytes=VMEM_LIMIT
+        ),
+        cost_estimate=pl.CostEstimate(
+            flops=2 * chunks * coefs * field_count * row_count * lon_total,
+            bytes_accessed=2 * grid_fields.size,
+            transcendentals=0,
+        ),
+        name="dft",
+    )(shift, ocos, osin, icos, isin, grid_fields, after)
+
+
+def turn_body(leg_ref, after_ref, out_ref, tail):
+    count, width, rows = leg_ref.shape
+    even = rows - 1
+    out_ref[: count * width, :] = leg_ref[:, :, :even].reshape(count * width, even)
+    lane = lax.broadcasted_iota(jnp.int32, (16, LANES), 1)
+    row = lax.broadcasted_iota(jnp.int32, (16, width), 0)
+    first = jnp.where(lane == 0, 1.0, 0.0).astype(BF16)
+    total = jnp.zeros((16, width), F32)
+    for slot in range(count):
+        column = jnp.broadcast_to(leg_ref[slot, :, even:].astype(F32), (width, LANES))
+        total = jnp.where(row == slot, nt_dot(first, column.astype(BF16)), total)
+    tail[...] = jnp.zeros_like(tail)
+    tail[:, :width] = total
+    out_ref[count * width :, :] = tail[...].astype(BF16)
+
+
+def turn_call(at, legendre, after):
+    width, rows = legendre.shape[1], legendre.shape[2]
+    out = (SLOTS * width + 16, rows - 1)
+    return pl.pallas_call(
+        turn_body,
+        grid=(1,),
+        in_specs=[
+            pl.BlockSpec((SLOTS, width, rows), lambda s: (at, 0, 0)),
+            pl.BlockSpec(memory_space=pl.ANY),
+        ],
+        out_specs=pl.BlockSpec(out, lambda s: (0, 0)),
+        out_shape=jax.ShapeDtypeStruct(out, BF16),
+        scratch_shapes=[pltpu.VMEM((16, rows - 1), F32)],
+        compiler_params=pltpu.CompilerParams(
+            dimension_semantics=("arbitrary",), vmem_limit_bytes=VMEM_LIMIT
+        ),
+        cost_estimate=pl.CostEstimate(
+            flops=2 * SLOTS * rows * width * width,
+            bytes_accessed=4 * SLOTS * rows * width,
+            transcendentals=0,
+        ),
+        name="turn",
+    )(legendre, after)
+
+
+def fold(arrived, sym, anti):
+    small = LANES // GROUP
+    halves = 4
+    groups = arrived.shape[1]
+    coefs = arrived.shape[3]
+    rows = lax.broadcasted_iota(jnp.int32, (LANES, LANES), 0)
+    columns = lax.broadcasted_iota(jnp.int32, (LANES, LANES), 1)
+    mirror = picks(rows, LANES - 1 - columns)
+    for lat in range(halves):
+        north = arrived[lat, :, :GROUP].reshape(groups * GROUP * coefs, LANES).astype(F32)
+        south = nn_dot(
+            arrived[2 * halves - 1 - lat, :, :GROUP].reshape(groups * GROUP * coefs, LANES), mirror
+        )
+        sym[lat] = (north + south).astype(BF16).astype(F32)
+        anti[lat] = (north - south).astype(BF16).astype(F32)
+    wide = halves * LANES
+    rows = lax.broadcasted_iota(jnp.int32, (wide, wide), 0)
+    columns = lax.broadcasted_iota(jnp.int32, (wide, wide), 1)
+    field, inside = columns // LANES, columns % LANES
+    lat, place = inside // small, inside % small
+    base = lat * LANES + field * small
+    north = nn_dot(
+        jnp.concatenate(
+            [arrived[at, :, GROUP].reshape(groups * coefs, LANES) for at in range(halves)], axis=1
+        ),
+        picks(rows, base + place),
+    )
+    south = nn_dot(
+        jnp.concatenate(
+            [
+                arrived[2 * halves - 1 - at, :, GROUP].reshape(groups * coefs, LANES)
+                for at in range(halves)
+            ],
+            axis=1,
+        ),
+        picks(rows, base + small - 1 - place),
+    )
+    both = (north + south).astype(BF16).astype(F32), (north - south).astype(BF16).astype(F32)
+    for group in range(groups):
+        for at in range(GROUP):
+            start = (group * GROUP + at) * coefs
+            for ref, values in zip((sym, anti), both):
+                ref[halves, start : start + coefs, :] = values[
+                    group * coefs : (group + 1) * coefs, at * LANES : (at + 1) * LANES
+                ]
+
+
+def level_body(
+    at, dims, pairs_ref, limits_ref, *refs
+):
+    field_count, wave_total, halves, fresh, piece = dims
+    parts, rest = refs[:8], refs[8:]
+    legendre, extra, one, two, three = rest[:5]
+    rest = rest[6:] if fresh else rest[7:]
+    spec_ref, outs, rest = rest[0], rest[1:9], rest[9:]
+    arrived, send_ref, sems, sym, anti, gathered, main_n, main_s, small_n, small_s = rest
+    slot = pl.program_id(0)
+    lat = limits_ref[3]
+    pair = pairs_ref[at * SLOTS + slot]
+    stride = 4 * SLOTS
+    both = 2 * field_count
+
+    @pl.when(slot == 0)
+    def _():
+        copies = [
+            pltpu.make_async_copy(parts[k].at[piece], arrived.at[jnp.bitwise_xor(lat, k)], sems.at[k])
+            for k in range(8)
+        ]
+        for copy in copies:
+            copy.start()
+        for copy in copies:
+            copy.wait()
+        fold(arrived, sym, anti)
+        for ref in (main_n, main_s, small_n, small_s):
+            ref[...] = jnp.zeros_like(ref)
+
+    def rows_of(ref):
+        return jnp.concatenate(
+            [
+                jnp.concatenate(
+                    [
+                        ref[tile, pl.ds(c * 2 * SLOTS + 2 * slot + w, field_count, stride=stride), :]
+                        for w in range(2)
+                        for c in range(2)
+                    ],
+                    axis=0,
+                )
+                for tile in range(ref.shape[0])
+            ],
+            axis=1,
+        )
+
+    sym_rows, anti_rows = rows_of(sym), rows_of(anti)
+    width = legendre.shape[1]
+    table = jnp.concatenate(
+        [legendre[g, :LANES, :] for g in range(4)] + [legendre[g, LANES:, :] for g in range(4)],
+        axis=0,
+    )
+    stacked = jnp.concatenate([sym_rows, anti_rows], axis=0).astype(BF16)
+    product = nn_dot(stacked, table)
+    row_at = lax.broadcasted_iota(jnp.int32, (16, 2 * LANES), 0)
+    lane_at = lax.broadcasted_iota(jnp.int32, (1, LANES), 1)
+    small = width - LANES
+    vector = []
+    last = jnp.zeros((1, LANES), F32)
+    for g in range(4):
+        line = jnp.sum(
+            jnp.where(row_at == slot, extra[g, :, : 2 * LANES].astype(F32), 0.0),
+            axis=0,
+            keepdims=True,
+        )
+        vector.append(line[:, :LANES])
+        moved = line[:, LANES:]
+        if g:
+            moved = pltpu.roll(moved, g * small, 1)
+        last = jnp.where(lane_at // small == g, moved, last)
+    vector = jnp.concatenate(vector + [last], axis=1)
+    final = jnp.sum(anti_rows * vector, axis=1, keepdims=True)
+
+    lanes = wave_total
+    rank = lax.broadcasted_iota(jnp.int32, (both, lanes), 1)
+    sym_count = wave_total // 2 + 1
+    sym_limit = (wave_total + 1 - pair) // 2
+    anti_limit = (wave_total - pair) // 2
+    spectrum = jnp.where(
+        rank < sym_count,
+        jnp.where(rank < sym_limit, product[:both], product[both : 2 * both]),
+        jnp.where(
+            rank < sym_count + anti_limit, product[2 * both : 3 * both], product[3 * both :]
+        ),
+    )
+    final = jnp.where(lanes - sym_count < anti_limit, final[:both], final[both:])
+    for tile in range(lanes // LANES):
+        gathered[tile, pl.ds(slot, both, stride=SLOTS), :] = spectrum[
+            :, tile * LANES : (tile + 1) * LANES
+        ]
+    gathered[lanes // LANES, pl.ds(slot, both, stride=SLOTS), :] = jnp.broadcast_to(
+        final, (both, LANES)
+    )
+    kept = spectrum.astype(BF16).astype(F32)
+
+    start = pl.multiple_of(slot * both, 16)
+    for level, (ref, offset) in enumerate(((one, 0), (two, 384), (three, 0))):
+        count = ref.shape[1]
+        half = count // 2
+        limit = limits_ref[level]
+        place = lax.broadcasted_iota(jnp.int32, (both, 512), 1)
+        first = jnp.where((place < half) & (pair + 2 * place <= limit), kept[:, :512], 0.0)
+        moved = pltpu.roll(kept[:, :512], 512 - (sym_count - half), 1)
+        second = jnp.where(
+            (place >= half) & (place < count) & (pair + 1 + 2 * (place - half) <= limit),
+            moved,
+            0.0,
+        )
+        halfway = nn_dot(
+            jnp.concatenate([first, second], axis=0)[:, :count].astype(BF16), ref[0]
+        )
+        even, odd = halfway[:both], halfway[both:]
+        if level < 2:
+            main_n[pl.ds(start, both), offset : offset + count] = (even + odd).astype(BF16)
+            main_s[pl.ds(start, both), offset : offset + count] = (even - odd).astype(BF16)
+        else:
+            small_n[pl.ds(start, both), :count] = even + odd
+            small_s[pl.ds(start, both), :count] = even - odd
+
+    @pl.when(slot == SLOTS - 1)
+    def _():
+        for c in range(2):
+            for tile in range(gathered.shape[0]):
+                size = LANES if tile < lanes // LANES else 1
+                spec_ref[:, c, :, tile * LANES : tile * LANES + size] = (
+                    gathered[tile, c * field_count * SLOTS : (c + 1) * field_count * SLOTS, :size]
+                    .astype(BF16)
+                    .reshape(field_count, SLOTS, size)
+                )
+        own = [2 * ref.shape[1] // 8 for ref in (one, two, three)]
+        wide = halves * LANES
+        for north, main, tiny in ((True, main_n, small_n), (False, main_s, small_s)):
+            rows = lax.broadcasted_iota(jnp.int32, (main.shape[1], wide), 0)
+            columns = lax.broadcasted_iota(jnp.int32, (main.shape[1], wide), 1)
+            owner, place = columns // LANES, columns % LANES
+            late = place - own[0]
+            if north:
+                first = owner * own[0] + place
+                second = 384 + owner * own[1] + late
+            else:
+                first = owner * own[0] + own[0] - 1 - place
+                second = 384 + owner * own[1] + own[1] - 1 - late
+            source = jnp.where(place < own[0], first, jnp.where(late < own[1], second, -1))
+            moved = nn_dot(main[...], picks(rows, source)).astype(BF16)
+            rows = lax.broadcasted_iota(jnp.int32, (LANES, wide), 0)
+            columns = lax.broadcasted_iota(jnp.int32, (LANES, wide), 1)
+            owner, place = columns // LANES, columns % LANES
+            block, inside = place // 64, place % 64
+            bundle, place = 3 * block + inside // own[2], inside % own[2]
+            bundle = jnp.where(inside < 3 * own[2], bundle, -1)
+            if not north:
+                place = own[2] - 1 - place
+            source = owner * own[2] + place
+            tiles = tiny[...].reshape(SLOTS, both // 8, 8, LANES)
+            packed = jnp.zeros((SLOTS * 8, wide), F32)
+            for g in range(both // 8):
+                packed = packed + nn_dot(
+                    tiles[:, g].reshape(SLOTS * 8, LANES).astype(BF16),
+                    picks(rows, jnp.where(bundle == g, source, -1)),
+                )
+            packed = packed.astype(BF16)
+            for owner in range(halves):
+                to = owner if north else 2 * halves - 1 - owner
+                lanes_at = slice(owner * LANES, (owner + 1) * LANES)
+                send_ref[to, : SLOTS * both, :] = moved[:, lanes_at]
+                send_ref[to, SLOTS * both :, :] = packed[:, lanes_at]
+        for k in range(8):
+            outs[k][...] = send_ref[jnp.bitwise_xor(lat, k)]
+
+
+def level_call(at, piece, pairs, limits, arrived, table, synths, after, spectrum, field_count):
+    wave_total = table.shape[2]
+    width = (table.shape[1] - 16) // SLOTS
+    both = 2 * field_count
+    fresh = spectrum is None
+    dims = (field_count, wave_total, 4, fresh, piece)
+    pair_local = pairs.shape[0]
+    spec_shape = (field_count, 2, pair_local, wave_total + 1)
+    rows = SLOTS * (both + 8)
+    operands = [pairs, limits, *arrived, table, table, *synths, after]
+    in_specs = [pl.BlockSpec(memory_space=pl.ANY) for _ in range(8)]
+    in_specs += [
+        pl.BlockSpec((4, width, wave_total), lambda s, *_: (0, s, 0)),
+        pl.BlockSpec((4, 16, wave_total), lambda s, *_: (0, SLOTS * width // 16, 0)),
+    ]
+    in_specs += [
+        pl.BlockSpec((1,) + ref.shape[1:], lambda s, *_: (at * SLOTS + s, 0, 0)) for ref in synths
+    ]
+    in_specs.append(pl.BlockSpec(memory_space=pl.ANY))
+    aliases = {}
+    if not fresh:
+        operands.append(spectrum)
+        in_specs.append(pl.BlockSpec(memory_space=pl.ANY))
+        aliases = {len(operands) - 1: 0}
+    flops = 2 * SLOTS * 4 * both * wave_total * wave_total
+    made = pl.pallas_call(
+        functools.partial(level_body, at, dims),
+        grid_spec=pltpu.PrefetchScalarGridSpec(
+            num_scalar_prefetch=2,
+            grid=(SLOTS,),
+            in_specs=in_specs,
+            out_specs=[
+                pl.BlockSpec(
+                    (field_count, 2, SLOTS, wave_total + 1), lambda s, *_: (0, 0, at, 0)
+                ),
+            ]
+            + [pl.BlockSpec((rows, LANES), lambda s, *_: (0, 0)) for _ in range(8)],
+            scratch_shapes=[
+                pltpu.VMEM((8,) + arrived[0].shape[1:], BF16),
+                pltpu.VMEM((8, rows, LANES), BF16),
+                pltpu.SemaphoreType.DMA((8,)),
+                pltpu.VMEM((5, field_count * 4 * SLOTS, LANES), F32),
+                pltpu.VMEM((5, field_count * 4 * SLOTS, LANES), F32),
+                pltpu.VMEM((wave_total // LANES + 1, both * SLOTS, LANES), F32),
+                pltpu.VMEM((SLOTS * both, 640), BF16),
+                pltpu.VMEM((SLOTS * both, 640), BF16),
+                pltpu.VMEM((SLOTS * both, LANES), F32),
+                pltpu.VMEM((SLOTS * both, LANES), F32),
+            ],
+        ),
+        out_shape=[jax.ShapeDtypeStruct(spec_shape, BF16)]
+        + [jax.ShapeDtypeStruct((rows, LANES), BF16)] * 8,
+        input_output_aliases=aliases,
+        compiler_params=pltpu.CompilerParams(
+            dimension_semantics=("arbitrary",), vmem_limit_bytes=VMEM_LIMIT
+        ),
+        cost_estimate=pl.CostEstimate(
+            flops=flops, bytes_accessed=2 * table.size, transcendentals=0
+        ),
+        name="levels",
+    )(*operands)
+    return made[0], made[1:]
+
+
+def inverse_body(chunks, field_step, lat_ref, *refs):
+    arrived = refs[: chunks * 8]
+    inv_one, inv_two, inv_three, out_one, out_two, out_three, main, tiny = refs[chunks * 8 :]
+    lat = lat_ref[3]
+    step = pl.program_id(0)
+    both = 2 * out_three.shape[1]
+    big = SLOTS * both
+    small = SLOTS * 8
+
+    @pl.when(step == 0)
+    def _():
+        for at in range(chunks):
+            for k in range(8):
+                place = at * 8 + jnp.bitwise_xor(lat, k)
+                part = arrived[at * 8 + k]
+                main[pl.ds(pl.multiple_of(place * big, 16), big), :] = part[:big, :].astype(F32)
+                tiny[pl.ds(pl.multiple_of(place * small, 16), small), :] = part[big:, :].astype(F32)
+
+    pairs = chunks * 8 * SLOTS
+    own = out_one.shape[1]
+    turned = []
+    for at in range(field_step):
+        field = step * field_step + at
+        rows = jnp.concatenate(
+            [main[pl.ds(c * (both // 2) + field, pairs, stride=both), :] for c in range(2)], axis=0
+        )
+        turned.append(rows.T.astype(BF16))
+    grid_rows = nn_dot(jnp.concatenate([x[:own] for x in turned], axis=0), inv_one[...])
+    for at in range(field_step):
+        out_one[at] = grid_rows[at * own : (at + 1) * own]
+    rest = LANES - own
+    grid_rows = nn_dot(jnp.concatenate([x[own:] for x in turned], axis=0), inv_two[...])
+    for at in range(field_step):
+        out_two[at] = grid_rows[at * rest : at * rest + out_two.shape[1]]
+
+    @pl.when(step < 4)
+    def _():
+        for at in range(2):
+            inside = 2 * step + at
+            rows = tiny[pl.ds(inside, pairs, stride=8), :]
+            turned = rows.T.astype(BF16)
+            grid_rows = nn_dot(turned[:64], inv_three[:pairs]) + nn_dot(
+                turned[64:], inv_three[pairs:]
+            )
+            count = out_three.shape[0]
+            for bundle in range(3):
+                for row in range(count):
+                    out_three[row, pl.ds(bundle * 8 + inside, 1), :] = grid_rows[
+                        bundle * count + row : bundle * count + row + 1
+                    ]
+
+
+def inverse_call(limits, arrived, tables, field_count):
+    chunks = len(arrived)
+    field_step = 4
+    both = 2 * field_count
+    whole = lambda shape: pl.BlockSpec(shape, lambda g, *_: (0,) * len(shape))
+    flat = [x for parts in arrived for x in parts]
+    outs = [(field_count, t.shape[1] // 16, t.shape[1]) for t in tables]
+    outs[2] = (outs[2][1], outs[2][0], outs[2][2])
+    one, two, three = pl.pallas_call(
+        functools.partial(inverse_body, chunks, field_step),
+        grid_spec=pltpu.PrefetchScalarGridSpec(
+            num_scalar_prefetch=1,
+            grid=(field_count // field_step,),
+            in_specs=[whole(x.shape) for x in flat] + [whole(t.shape) for t in tables],
+            out_specs=[
+                pl.BlockSpec((field_step,) + outs[0][1:], lambda g, *_: (g, 0, 0)),
+                pl.BlockSpec((field_step,) + outs[1][1:], lambda g, *_: (g, 0, 0)),
+                whole(outs[2]),
+            ],
+            scratch_shapes=[
+                pltpu.VMEM((chunks * 8 * SLOTS * both, LANES), F32),
+                pltpu.VMEM((chunks * 8 * SLOTS * 8, LANES), F32),
+            ],
+        ),
+        out_shape=[jax.ShapeDtypeStruct(shape, F32) for shape in outs],
+        compiler_params=pltpu.CompilerParams(
+            dimension_semantics=("arbitrary",), vmem_limit_bytes=VMEM_LIMIT
+        ),
+        cost_estimate=pl.CostEstimate(
+            flops=2 * field_count * LANES * both * 640, bytes_accessed=1 << 24, transcendentals=0
+        ),
+        name="inverse",
+    )(limits, *flat, *tables)
+    return one, two, three.transpose(1, 0, 2)
+
+
+def wave_trig(waves, length):
+    step = 2.0 * math.pi / length
+
+    def angles(places):
+        return ((places[:, None] * waves[None, :]) % length).astype(F32) * step
+
+    outer = angles(jnp.arange(length // LANES, dtype=jnp.int32) * LANES)
+    inner = angles(jnp.arange(LANES, dtype=jnp.int32))
+    return jnp.cos(outer), jnp.sin(outer), jnp.cos(inner), jnp.sin(inner)
+
+
+def chunked_on_device(grid_fields, assign, limits, legendre, synth_one, synth_two, synth_three):
+    lat_count = lax.axis_size("lat")
+    field_count, row_count, lon_total = grid_fields.shape
+    pair_total = assign.shape[0]
+    pair_local = pair_total // lat_count
+    wave_total = 2 * pair_total
+    chunks = pair_local // SLOTS
+    synths = (synth_one, synth_two, synth_three)
+    lat = lax.axis_index("lat")
+    by_owner = assign.reshape(lat_count, chunks, SLOTS)
+    own_pairs = lax.dynamic_slice(assign, (lat * pair_local,), (pair_local,))
+    south = (lat >= lat_count // 2).astype(jnp.int32)
+    small = row_count - LANES
+    shift = jnp.stack([south * small, (1 - south) * LANES])
+
+    scalars = jnp.concatenate([limits, lat.astype(jnp.int32)[None]])
+    partners = jnp.bitwise_xor(lat, jnp.arange(lat_count, dtype=jnp.int32))
+    to_partner = jnp.take(by_owner, partners, axis=0)
+    turned = legendre.transpose(0, 2, 1)
+    waves = jnp.stack([to_partner, wave_total - 1 - to_partner], axis=3)
+    waves = waves.transpose(1, 0, 2, 3).reshape(chunks, -1)
+
+    def exchange(parts):
+        return [parts[0]] + [
+            lax.ppermute(parts[k], "lat", [(i, i ^ k) for i in range(lat_count)])
+            for k in range(1, lat_count)
+        ]
+
+    def gather(at, after):
+        packed = turn_call(at, turned, after)
+        return packed, lax.all_gather(packed, "fld")
+
+    spans = [(0, 1)] + [(at, min(at + 2, chunks)) for at in range(1, chunks, 2)]
+    packed, table = gather(0, assign)
+    tables = [table]
+    crossed = []
+    after = packed
+    for first, last in spans:
+        trig = wave_trig(waves[first:last].reshape(-1), lon_total)
+        sent = dft_call(shift, trig, grid_fields, after)
+        after = sent[0]
+        moved = exchange(sent)
+        crossed += [(moved, piece) for piece in range(last - first)]
+        tables += [gather(chunk, after)[1] for chunk in range(max(first, 1), last)]
+
+    order = by_owner.transpose(1, 0, 2).reshape(-1)
+    inverses = [both_parts(order, 4 * table.shape[1]) for table in synths]
+    spectrum = None
+    arrived = []
+    for at in range(chunks):
+        after = inverses[at % 3]
+        moved, piece = crossed[at]
+        spectrum, send = level_call(
+            at, piece, own_pairs, scalars, moved, tables[at], synths, after, spectrum, field_count
+        )
+        arrived.append(exchange(send))
+    return (spectrum, *inverse_call(scalars, arrived, inverses, field_count))
+
+
+def both_parts(order, length):
+    weight = jnp.where(order == 0, 1.0, 2.0).astype(F32) / math.sqrt(length)
+    waves = jnp.concatenate([order, order])
+    quarters = jnp.concatenate([jnp.zeros_like(order), jnp.ones_like(order)])
+    table = turned_cosine(waves, quarters, jnp.arange(length, dtype=jnp.int32))
+    return (table * jnp.concatenate([weight, weight])[:, None]).astype(BF16)
+
+
+def on_device(*arguments):
+    if fits(*arguments):
+        return chunked_on_device(*arguments)
+    return plain_on_device(*arguments)
+
+
 def solution(mesh):
     return jax.shard_map(
         on_device,

time: 718 us -> 521 us (0.73)
  the two profiles are of different devices: /device:TPU:0 before, /device:TPU:8 now
where the time goes in v1:
time: 521 us; the launch traced here: 511 us
  Pallas kernels  183 us (35%)
  waiting for transfers between devices  180 us (35%)
  starting transfers between devices  102 us (20%)
  other arithmetic  21.2 us (4%)
  between operations  15.4 us (3%)
  local copies, waits for them, and re-layouts  9.08 us (2%)
    ppermute x56, waiting for transfers between devices, exchange(): lax.ppermute(parts[k], 'lat', [(i, i ^ k) for i in range(lat_count)])  179 us
    ppermute x56, starting transfers between devices, exchange(): lax.ppermute(parts[k], 'lat', [(i, i ^ k) for i in range(lat_count)])  90 us
    pallas_call x3, Pallas kernels, dft_call(): pl.pallas_call(functools.partial(dft_body, chunks, 1.0 / math.sqrt(lon_to...  76.6 us
    pallas_call x5, Pallas kernels, level_call(): pl.pallas_call(functools.partial(level_body, at, dims), grid_spec=pltpu.P...  74.7 us
    pallas_call x1, Pallas kernels, inverse_call(): pl.pallas_call(functools.partial(inverse_body, chunks, field_step), grid_...  16.3 us
    pallas_call x5, Pallas kernels, turn_call(): pl.pallas_call(turn_body, grid=(1,), in_specs=[pl.BlockSpec((SLOTS, width...  15.5 us
    all_gather x5, starting transfers between devices, gather(): return (packed, lax.all_gather(packed, 'fld'))  12.2 us
  transfers between devices with their start and end apart: 61, of which 21 were waited for; matrix products, arithmetic and copies ran while one was open for 6% of the time, Pallas kernels for 32%

profile of v1, /device:TPU:8, one launch (start us, length us, event | category | flops | bytes accessed | tf_op | source)
XLA Modules:
  0.0 510.6 jit_solution(16451102250263059558)
XLA Ops:
  16.6 15.1 %dft.3 = (bf16[1,6,5,32,128]{4,3,2,1,0:T(8,128)(2,1)}, bf16[1,6,5,32,128]{4,3,2,1,0:T(8,128)(2,1)}, bf16[1,6,5,32,128]{4,3,2,1,0:T(8,128)(2,1)}, bf16[1,6,5,32,1...) custom-call(s32[2]{0:T(128)} %pad_add_fusion.2.shift_ref, ...), custom_call_target="tpu_custom_call" | custom-call | flops 5033164800 | bytes 19660800 | tf_op jit(solution)/shard_map/dft/pallas_call | solution.py:319
  31.7 30.7 %dft.4 = (bf16[2,6,5,32,128]{4,3,2,1,0:T(8,128)(2,1)}, bf16[2,6,5,32,128]{4,3,2,1,0:T(8,128)(2,1)}, bf16[2,6,5,32,128]{4,3,2,1,0:T(8,128)(2,1)}, bf16[2,6,5,32,1...) custom-call(s32[2]{0:T(128)} %pad_add_fusion.2.shift_ref, ...), custom_call_target="tpu_custom_call" | custom-call | flops 10066329600 | bytes 19660800 | tf_op jit(solution)/shard_map/dft/pallas_call | solution.py:319
  70.0 30.8 %dft.5 = (bf16[2,6,5,32,128]{4,3,2,1,0:T(8,128)(2,1)}, bf16[2,6,5,32,128]{4,3,2,1,0:T(8,128)(2,1)}, bf16[2,6,5,32,128]{4,3,2,1,0:T(8,128)(2,1)}, bf16[2,6,5,32,1...) custom-call(s32[2]{0:T(128)} %pad_add_fusion.2.shift_ref, ...), custom_call_target="tpu_custom_call" | custom-call | flops 10066329600 | bytes 19660800 | tf_op jit(solution)/shard_map/dft/pallas_call | solution.py:319
  104.0 12.0 %all-gather.11.cloned.1.call-start = ((), (), s32[]{:S(2)}) async-start(), calls=%async_computation | async-start | bytes 8294400 | tf_op jit(solution)/shard_map/all_gather | solution.py:806
  150.0 6.8 %collective-permute-start.10 = (bf16[2,6,5,32,128]{4,3,2,1,0:T(8,128)(2,1)S(1)}, bf16[2,6,5,32,128]{4,3,2,1,0:T(8,128)(2,1)S(1)}, u32[]{:S(2)}, u32[]{:S(2)}) collective-permute-start(bf16[2,6,5,32,128]{4,3,2,1,0:T(8,128)(2,1)S(1)} %copy-done.60), channel_id=1, source_target_pairs={{0,16},{4,20},{8,24},{12,28},{16,0},{20,4},{24,8},{28,12},{1,17},{... | collective-permute-start | bytes 1474568 | tf_op jit(solution)/shard_map/ppermute | solution.py:800
  157.5 3.9 collective-permute-start.20
  161.6 28.4 %collective-permute-done.20.refs_7_ = bf16[1,6,5,32,128]{4,3,2,1,0:T(8,128)(2,1)S(1)} collective-permute-done((bf16[1,6,5,32,128]{4,3,2,1,0:T(8,128)(2,1)S(1)}, bf16[1,6,5,32,128]{4,3,2,1,0:T(8,128)(2,1)S(1)}, u32[]{:S(2)}, u32[]{:S(2)}) %collective-permute-start.20) | collective-permute-done | bytes 245792 | tf_op jit(solution)/shard_map/ppermute | solution.py:800
  190.0 8.8 %collective-permute-start.11 = (bf16[2,6,5,32,128]{4,3,2,1,0:T(8,128)(2,1)S(1)}, bf16[2,6,5,32,128]{4,3,2,1,0:T(8,128)(2,1)S(1)}, u32[]{:S(2)}, u32[]{:S(2)}) collective-permute-start(bf16[2,6,5,32,128]{4,3,2,1,0:T(8,128)(2,1)S(1)} %copy-done.58), channel_id=1, source_target_pairs={{0,20},{4,16},{8,28},{12,24},{16,4},{20,0},{24,12},{28,8},{1,21},{... | collective-permute-start | bytes 1474568 | tf_op jit(solution)/shard_map/ppermute | solution.py:800
  204.8 30.3 %collective-permute-done.11.refs_5_ = bf16[2,6,5,32,128]{4,3,2,1,0:T(8,128)(2,1)S(1)} collective-permute-done((bf16[2,6,5,32,128]{4,3,2,1,0:T(8,128)(2,1)S(1)}, bf16[2,6,5,32,128]{4,3,2,1,0:T(8,128)(2,1)S(1)}, u32[]{:S(2)}, u32[]{:S(2)}) %collective-permute-start.11) | collective-permute-done | bytes 491552 | tf_op jit(solution)/shard_map/ppermute | solution.py:800
  235.0 3.6 collective-permute-start.2
  238.6 8.2 %collective-permute-done.12.refs_6_ = bf16[2,6,5,32,128]{4,3,2,1,0:T(8,128)(2,1)S(1)} collective-permute-done((bf16[2,6,5,32,128]{4,3,2,1,0:T(8,128)(2,1)S(1)}, bf16[2,6,5,32,128]{4,3,2,1,0:T(8,128)(2,1)S(1)}, u32[]{:S(2)}, u32[]{:S(2)}) %collective-permute-start.12) | collective-permute-done | bytes 491552 | tf_op jit(solution)/shard_map/ppermute | solution.py:800
  246.8 24.9 %collective-permute-done.13.refs_7_ = bf16[2,6,5,32,128]{4,3,2,1,0:T(8,128)(2,1)S(1)} collective-permute-done((bf16[2,6,5,32,128]{4,3,2,1,0:T(8,128)(2,1)S(1)}, bf16[2,6,5,32,128]{4,3,2,1,0:T(8,128)(2,1)S(1)}, u32[]{:S(2)}, u32[]{:S(2)}) %collective-permute-start.13) | collective-permute-done | bytes 491552 | tf_op jit(solution)/shard_map/ppermute | solution.py:800
  274.2 14.8 %levels.5 = (bf16[24,2,40,641]{3,2,1,0:T(8,128)(2,1)}, bf16[448,128]{1,0:T(8,128)(2,1)}, bf16[448,128]{1,0:T(8,128)(2,1)}, bf16[448,128]{1,0:T(8,128)(2,1)}, bf1...) custom-call(s32[40]{0:T(128)} %dynamic_slice.3.pairs_ref, ...), custom_call_target="tpu_custom_call" | custom-call | flops 1258291200 | bytes 6635520 | tf_op jit(solution)/shard_map/levels/pallas_call | solution.py:638
  292.0 18.3 %collective-permute-done.3.refs_4_ = bf16[2,6,5,32,128]{4,3,2,1,0:T(8,128)(2,1)S(1)} collective-permute-done((bf16[2,6,5,32,128]{4,3,2,1,0:T(8,128)(2,1)}, bf16[2,6,5,32,128]{4,3,2,1,0:T(8,128)(2,1)S(1)}, u32[]{:S(2)}, u32[]{:S(2)}) %collective-permute-start.3) | collective-permute-done | bytes 491552 | tf_op jit(solution)/shard_map/ppermute | solution.py:800
  312.6 8.3 %collective-permute-done.4.refs_5_ = bf16[2,6,5,32,128]{4,3,2,1,0:T(8,128)(2,1)S(1)} collective-permute-done((bf16[2,6,5,32,128]{4,3,2,1,0:T(8,128)(2,1)}, bf16[2,6,5,32,128]{4,3,2,1,0:T(8,128)(2,1)S(1)}, u32[]{:S(2)}, u32[]{:S(2)}) %collective-permute-start.4) | collective-permute-done | bytes 491552 | tf_op jit(solution)/shard_map/ppermute | solution.py:800
  324.1 8.2 %collective-permute-done.5.refs_6_ = bf16[2,6,5,32,128]{4,3,2,1,0:T(8,128)(2,1)S(1)} collective-permute-done((bf16[2,6,5,32,128]{4,3,2,1,0:T(8,128)(2,1)}, bf16[2,6,5,32,128]{4,3,2,1,0:T(8,128)(2,1)S(1)}, u32[]{:S(2)}, u32[]{:S(2)}) %collective-permute-start.5) | collective-permute-done | bytes 491552 | tf_op jit(solution)/shard_map/ppermute | solution.py:800
  332.3 15.2 %collective-permute-done.6.refs_7_ = bf16[2,6,5,32,128]{4,3,2,1,0:T(8,128)(2,1)S(1)} collective-permute-done((bf16[2,6,5,32,128]{4,3,2,1,0:T(8,128)(2,1)}, bf16[2,6,5,32,128]{4,3,2,1,0:T(8,128)(2,1)S(1)}, u32[]{:S(2)}, u32[]{:S(2)}) %collective-permute-start.6) | collective-permute-done | bytes 491552 | tf_op jit(solution)/shard_map/ppermute | solution.py:800
  347.5 14.9 %levels.6 = (bf16[24,2,40,641]{3,2,1,0:T(8,128)(2,1)}, bf16[448,128]{1,0:T(8,128)(2,1)}, bf16[448,128]{1,0:T(8,128)(2,1)}, bf16[448,128]{1,0:T(8,128)(2,1)}, bf1...) custom-call(s32[40]{0:T(128)} %dynamic_slice.3.pairs_ref, ...), custom_call_target="tpu_custom_call", output_to_operand_aliasing={{0}: (16, {})} | custom-call | flops 1258291200 | bytes 6635520 | tf_op jit(solution)/shard_map/levels/pallas_call | solution.py:638
  362.9 3.2 collective-permute-start.28
  366.1 3.5 collective-permute-start.29
  369.7 15.1 %levels.7 = (bf16[24,2,40,641]{3,2,1,0:T(8,128)(2,1)}, bf16[448,128]{1,0:T(8,128)(2,1)}, bf16[448,128]{1,0:T(8,128)(2,1)}, bf16[448,128]{1,0:T(8,128)(2,1)}, bf1...) custom-call(s32[40]{0:T(128)} %dynamic_slice.3.pairs_ref, ...), custom_call_target="tpu_custom_call", output_to_operand_aliasing={{0}: (16, {})} | custom-call | flops 1258291200 | bytes 6635520 | tf_op jit(solution)/shard_map/levels/pallas_call | solution.py:638
  384.9 4.2 collective-permute-start.31
  392.8 6.8 %collective-permute-done.31.refs_12_ = bf16[448,128]{1,0:T(8,128)(2,1)S(1)} collective-permute-done((bf16[448,128]{1,0:T(8,128)(2,1)S(1)}, bf16[448,128]{1,0:T(8,128)(2,1)S(1)}, u32[]{:S(2)}, u32[]{:S(2)}) %collective-permute-start.31) | collective-permute-done | bytes 114720 | tf_op jit(solution)/shard_map/ppermute | solution.py:800
  405.3 4.6 collective-permute-done.34.refs_15_
  410.1 14.9 %levels.8 = (bf16[24,2,40,641]{3,2,1,0:T(8,128)(2,1)}, bf16[448,128]{1,0:T(8,128)(2,1)}, bf16[448,128]{1,0:T(8,128)(2,1)}, bf16[448,128]{1,0:T(8,128)(2,1)}, bf1...) custom-call(s32[40]{0:T(128)} %dynamic_slice.3.pairs_ref, ...), custom_call_target="tpu_custom_call", output_to_operand_aliasing={{0}: (16, {})} | custom-call | flops 1258291200 | bytes 6635520 | tf_op jit(solution)/shard_map/levels/pallas_call | solution.py:638
  432.0 4.2 collective-permute-start.45
  436.3 14.9 %levels.9 = (bf16[24,2,40,641]{3,2,1,0:T(8,128)(2,1)}, bf16[448,128]{1,0:T(8,128)(2,1)}, bf16[448,128]{1,0:T(8,128)(2,1)}, bf16[448,128]{1,0:T(8,128)(2,1)}, bf1...) custom-call(s32[40]{0:T(128)} %dynamic_slice.3.pairs_ref, ...), custom_call_target="tpu_custom_call", output_to_operand_aliasing={{0}: (16, {})} | custom-call | flops 1258291200 | bytes 6635520 | tf_op jit(solution)/shard_map/levels/pallas_call | solution.py:638
  457.5 3.4 collective-permute-done.46.refs_29_
  465.3 4.2 collective-permute-done.48.refs_31_
  472.0 4.6 collective-permute-done.52.refs_36_
  479.1 5.4 %collective-permute-done.54.refs_38_ = bf16[448,128]{1,0:T(8,128)(2,1)S(1)} collective-permute-done((bf16[448,128]{1,0:T(8,128)(2,1)}, bf16[448,128]{1,0:T(8,128)(2,1)S(1)}, u32[]{:S(2)}, u32[]{:S(2)}) %collective-permute-start.54) | collective-permute-done | bytes 114720 | tf_op jit(solution)/shard_map/ppermute | solution.py:800
  487.4 16.3 %inverse.1 = (f32[24,80,1280]{2,1,0:T(8,128)}, f32[24,40,640]{2,1,0:T(8,128)}, f32[20,24,320]{2,1,0:T(8,128)}) custom-call(s32[4]{0:T(128)} %pad_add_fusion.1.limits_ref.lat_ref, bf16[448,128]{1,0:T(8,128)(2,1)} %get-tuple-element.129.refs_0_, bf16[448,128]{1,0:T(8,128)(2,1)} %copy-done.17, bf16[448,128]{1,0:T(8,128)(2,1)} %copy-done.18, ...), custom_call_target="tpu_custom_call" | custom-call | flops 188743680 | bytes 16777216 | tf_op jit(solution)/shard_map/inverse/pallas_call | solution.py:737
  (329 shorter events, 106.7 us)
Async XLA Ops:
  7.2 267.0 %all-gather.19.cloned.1.call-start = ((), (), s32[]{:S(2)}) async-start(), calls=%async_computation.4 | async-start | bytes 8294400 | tf_op jit(solution)/shard_map/all_gather | solution.py:806
  10.3 337.1 %all-gather.17.cloned.1.call-start = ((), (), s32[]{:S(2)}) async-start(), calls=%async_computation.3 | async-start | bytes 8294400 | tf_op jit(solution)/shard_map/all_gather | solution.py:806
  65.6 304.1 %all-gather.15.cloned.1.call-start = ((), (), s32[]{:S(2)}) async-start(), calls=%async_computation.2 | async-start | bytes 8294400 | tf_op jit(solution)/shard_map/all_gather | solution.py:806
  68.7 341.3 %all-gather.13.cloned.1.call-start = ((), (), s32[]{:S(2)}) async-start(), calls=%async_computation.1 | async-start | bytes 8294400 | tf_op jit(solution)/shard_map/all_gather | solution.py:806
  104.0 332.3 %all-gather.11.cloned.1.call-start = ((), (), s32[]{:S(2)}) async-start(), calls=%async_computation | async-start | bytes 8294400 | tf_op jit(solution)/shard_map/all_gather | solution.py:806
  119.1 25.0 %collective-permute-start.14 = (bf16[1,6,5,32,128]{4,3,2,1,0:T(8,128)(2,1)}, bf16[1,6,5,32,128]{4,3,2,1,0:T(8,128)(2,1)S(1)}, u32[]{:S(2)}, u32[]{:S(2)}) collective-permute-start(bf16[1,6,5,32,128]{4,3,2,1,0:T(8,128)(2,1)} %get-tuple-element.117), channel_id=1, source_target_pairs={{0,4},{4,0},{8,12},{12,8},{16,20},{20,16},{24,28},{28,24},{1,5},{5... | collective-permute-start | bytes 737288 | tf_op jit(solution)/shard_map/ppermute | solution.py:800
  120.6 25.1 %collective-permute-start.15 = (bf16[1,6,5,32,128]{4,3,2,1,0:T(8,128)(2,1)}, bf16[1,6,5,32,128]{4,3,2,1,0:T(8,128)(2,1)}, u32[]{:S(2)}, u32[]{:S(2)}) collective-permute-start(bf16[1,6,5,32,128]{4,3,2,1,0:T(8,128)(2,1)} %get-tuple-element.118), channel_id=1, source_target_pairs={{0,8},{4,12},{8,0},{12,4},{16,24},{20,28},{24,16},{28,20},{1,9},{5... | collective-permute-start | bytes 737288 | tf_op jit(solution)/shard_map/ppermute | solution.py:800
  121.3 25.1 %collective-permute-start.16 = (bf16[1,6,5,32,128]{4,3,2,1,0:T(8,128)(2,1)}, bf16[1,6,5,32,128]{4,3,2,1,0:T(8,128)(2,1)}, u32[]{:S(2)}, u32[]{:S(2)}) collective-permute-start(bf16[1,6,5,32,128]{4,3,2,1,0:T(8,128)(2,1)} %get-tuple-element.119), channel_id=1, source_target_pairs={{0,12},{4,8},{8,4},{12,0},{16,28},{20,24},{24,20},{28,16},{1,13},{... | collective-permute-start | bytes 737288 | tf_op jit(solution)/shard_map/ppermute | solution.py:800
  122.7 26.0 %collective-permute-start.17 = (bf16[1,6,5,32,128]{4,3,2,1,0:T(8,128)(2,1)}, bf16[1,6,5,32,128]{4,3,2,1,0:T(8,128)(2,1)}, u32[]{:S(2)}, u32[]{:S(2)}) collective-permute-start(bf16[1,6,5,32,128]{4,3,2,1,0:T(8,128)(2,1)} %get-tuple-element.120), channel_id=1, source_target_pairs={{0,16},{4,20},{8,24},{12,28},{16,0},{20,4},{24,8},{28,12},{1,17},{... | collective-permute-start | bytes 737288 | tf_op jit(solution)/shard_map/ppermute | solution.py:800
  145.8 53.0 %collective-permute-start.7 = (bf16[2,6,5,32,128]{4,3,2,1,0:T(8,128)(2,1)S(1)}, bf16[2,6,5,32,128]{4,3,2,1,0:T(8,128)(2,1)S(1)}, u32[]{:S(2)}, u32[]{:S(2)}) collective-permute-start(bf16[2,6,5,32,128]{4,3,2,1,0:T(8,128)(2,1)S(1)} %copy-done.64), channel_id=1, source_target_pairs={{0,4},{4,0},{8,12},{12,8},{16,20},{20,16},{24,28},{28,24},{1,5},{5... | collective-permute-start | bytes 1474568 | tf_op jit(solution)/shard_map/ppermute | solution.py:800
  146.3 52.6 %collective-permute-start.8 = (bf16[2,6,5,32,128]{4,3,2,1,0:T(8,128)(2,1)S(1)}, bf16[2,6,5,32,128]{4,3,2,1,0:T(8,128)(2,1)S(1)}, u32[]{:S(2)}, u32[]{:S(2)}) collective-permute-start(bf16[2,6,5,32,128]{4,3,2,1,0:T(8,128)(2,1)S(1)} %copy-done.63), channel_id=1, source_target_pairs={{0,8},{4,12},{8,0},{12,4},{16,24},{20,28},{24,16},{28,20},{1,9},{5... | collective-permute-start | bytes 1474568 | tf_op jit(solution)/shard_map/ppermute | solution.py:800
  148.7 51.3 %collective-permute-start.9 = (bf16[2,6,5,32,128]{4,3,2,1,0:T(8,128)(2,1)S(1)}, bf16[2,6,5,32,128]{4,3,2,1,0:T(8,128)(2,1)S(1)}, u32[]{:S(2)}, u32[]{:S(2)}) collective-permute-start(bf16[2,6,5,32,128]{4,3,2,1,0:T(8,128)(2,1)S(1)} %copy-done.62), channel_id=1, source_target_pairs={{0,12},{4,8},{8,4},{12,0},{16,28},{20,24},{24,20},{28,16},{1,13},{... | collective-permute-start | bytes 1474568 | tf_op jit(solution)/shard_map/ppermute | solution.py:800
  150.0 52.5 %collective-permute-start.10 = (bf16[2,6,5,32,128]{4,3,2,1,0:T(8,128)(2,1)S(1)}, bf16[2,6,5,32,128]{4,3,2,1,0:T(8,128)(2,1)S(1)}, u32[]{:S(2)}, u32[]{:S(2)}) collective-permute-start(bf16[2,6,5,32,128]{4,3,2,1,0:T(8,128)(2,1)S(1)} %copy-done.60), channel_id=1, source_target_pairs={{0,16},{4,20},{8,24},{12,28},{16,0},{20,4},{24,8},{28,12},{1,17},{... | collective-permute-start | bytes 1474568 | tf_op jit(solution)/shard_map/ppermute | solution.py:800
  157.5 32.5 %collective-permute-start.20 = (bf16[1,6,5,32,128]{4,3,2,1,0:T(8,128)(2,1)S(1)}, bf16[1,6,5,32,128]{4,3,2,1,0:T(8,128)(2,1)S(1)}, u32[]{:S(2)}, u32[]{:S(2)}) collective-permute-start(bf16[1,6,5,32,128]{4,3,2,1,0:T(8,128)(2,1)S(1)} %copy-done.65), channel_id=1, source_target_pairs={{0,28},{4,24},{8,20},{12,16},{16,12},{20,8},{24,4},{28,0},{1,29},{... | collective-permute-start | bytes 737288 | tf_op jit(solution)/shard_map/ppermute | solution.py:800
  190.0 45.0 %collective-permute-start.11 = (bf16[2,6,5,32,128]{4,3,2,1,0:T(8,128)(2,1)S(1)}, bf16[2,6,5,32,128]{4,3,2,1,0:T(8,128)(2,1)S(1)}, u32[]{:S(2)}, u32[]{:S(2)}) collective-permute-start(bf16[2,6,5,32,128]{4,3,2,1,0:T(8,128)(2,1)S(1)} %copy-done.58), channel_id=1, source_target_pairs={{0,20},{4,16},{8,28},{12,24},{16,4},{20,0},{24,12},{28,8},{1,21},{... | collective-permute-start | bytes 1474568 | tf_op jit(solution)/shard_map/ppermute | solution.py:800
  198.8 48.0 %collective-permute-start.12 = (bf16[2,6,5,32,128]{4,3,2,1,0:T(8,128)(2,1)S(1)}, bf16[2,6,5,32,128]{4,3,2,1,0:T(8,128)(2,1)S(1)}, u32[]{:S(2)}, u32[]{:S(2)}) collective-permute-start(bf16[2,6,5,32,128]{4,3,2,1,0:T(8,128)(2,1)S(1)} %copy-done.57), channel_id=1, source_target_pairs={{0,24},{4,28},{8,16},{12,20},{16,8},{20,12},{24,0},{28,4},{1,25},{... | collective-permute-start | bytes 1474568 | tf_op jit(solution)/shard_map/ppermute | solution.py:800
  198.9 72.8 %collective-permute-start.13 = (bf16[2,6,5,32,128]{4,3,2,1,0:T(8,128)(2,1)S(1)}, bf16[2,6,5,32,128]{4,3,2,1,0:T(8,128)(2,1)S(1)}, u32[]{:S(2)}, u32[]{:S(2)}) collective-permute-start(bf16[2,6,5,32,128]{4,3,2,1,0:T(8,128)(2,1)S(1)} %copy-done.56), channel_id=1, source_target_pairs={{0,28},{4,24},{8,20},{12,16},{16,12},{20,8},{24,4},{28,0},{1,29},{... | collective-permute-start | bytes 1474568 | tf_op jit(solution)/shard_map/ppermute | solution.py:800
  200.0 71.8 %collective-permute-start = (bf16[2,6,5,32,128]{4,3,2,1,0:T(8,128)(2,1)S(1)}, bf16[2,6,5,32,128]{4,3,2,1,0:T(8,128)(2,1)S(1)}, u32[]{:S(2)}, u32[]{:S(2)}) collective-permute-start(bf16[2,6,5,32,128]{4,3,2,1,0:T(8,128)(2,1)S(1)} %copy-done.61), channel_id=1, source_target_pairs={{0,4},{4,0},{8,12},{12,8},{16,20},{20,16},{24,28},{28,24},{1,5},{5... | collective-permute-start | bytes 1474568 | tf_op jit(solution)/shard_map/ppermute | solution.py:800
  203.3 68.6 %collective-permute-start.1 = (bf16[2,6,5,32,128]{4,3,2,1,0:T(8,128)(2,1)S(1)}, bf16[2,6,5,32,128]{4,3,2,1,0:T(8,128)(2,1)S(1)}, u32[]{:S(2)}, u32[]{:S(2)}) collective-permute-start(bf16[2,6,5,32,128]{4,3,2,1,0:T(8,128)(2,1)S(1)} %copy-done.59), channel_id=1, source_target_pairs={{0,8},{4,12},{8,0},{12,4},{16,24},{20,28},{24,16},{28,20},{1,9},{5... | collective-permute-start | bytes 1474568 | tf_op jit(solution)/shard_map/ppermute | solution.py:800
  235.0 53.9 %collective-permute-start.2 = (bf16[2,6,5,32,128]{4,3,2,1,0:T(8,128)(2,1)}, bf16[2,6,5,32,128]{4,3,2,1,0:T(8,128)(2,1)S(1)}, u32[]{:S(2)}, u32[]{:S(2)}) collective-permute-start(bf16[2,6,5,32,128]{4,3,2,1,0:T(8,128)(2,1)} %get-tuple-element.93), channel_id=1, source_target_pairs={{0,12},{4,8},{8,4},{12,0},{16,28},{20,24},{24,20},{28,16},{1,13},{... | collective-permute-start | bytes 1474568 | tf_op jit(solution)/shard_map/ppermute | solution.py:800
  246.8 63.5 %collective-permute-start.3 = (bf16[2,6,5,32,128]{4,3,2,1,0:T(8,128)(2,1)}, bf16[2,6,5,32,128]{4,3,2,1,0:T(8,128)(2,1)S(1)}, u32[]{:S(2)}, u32[]{:S(2)}) collective-permute-start(bf16[2,6,5,32,128]{4,3,2,1,0:T(8,128)(2,1)} %get-tuple-element.94), channel_id=1, source_target_pairs={{0,16},{4,20},{8,24},{12,28},{16,0},{20,4},{24,8},{28,12},{1,17},{... | collective-permute-start | bytes 1474568 | tf_op jit(solution)/shard_map/ppermute | solution.py:800
  271.7 49.2 %collective-permute-start.4 = (bf16[2,6,5,32,128]{4,3,2,1,0:T(8,128)(2,1)}, bf16[2,6,5,32,128]{4,3,2,1,0:T(8,128)(2,1)S(1)}, u32[]{:S(2)}, u32[]{:S(2)}) collective-permute-start(bf16[2,6,5,32,128]{4,3,2,1,0:T(8,128)(2,1)} %get-tuple-element.95), channel_id=1, source_target_pairs={{0,20},{4,16},{8,28},{12,24},{16,4},{20,0},{24,12},{28,8},{1,21},{... | collective-permute-start | bytes 1474568 | tf_op jit(solution)/shard_map/ppermute | solution.py:800
  271.8 60.4 %collective-permute-start.5 = (bf16[2,6,5,32,128]{4,3,2,1,0:T(8,128)(2,1)}, bf16[2,6,5,32,128]{4,3,2,1,0:T(8,128)(2,1)S(1)}, u32[]{:S(2)}, u32[]{:S(2)}) collective-permute-start(bf16[2,6,5,32,128]{4,3,2,1,0:T(8,128)(2,1)} %get-tuple-element.96), channel_id=1, source_target_pairs={{0,24},{4,28},{8,16},{12,20},{16,8},{20,12},{24,0},{28,4},{1,25},{... | collective-permute-start | bytes 1474568 | tf_op jit(solution)/shard_map/ppermute | solution.py:800
  272.0 75.5 %collective-permute-start.6 = (bf16[2,6,5,32,128]{4,3,2,1,0:T(8,128)(2,1)}, bf16[2,6,5,32,128]{4,3,2,1,0:T(8,128)(2,1)S(1)}, u32[]{:S(2)}, u32[]{:S(2)}) collective-permute-start(bf16[2,6,5,32,128]{4,3,2,1,0:T(8,128)(2,1)} %get-tuple-element.97), channel_id=1, source_target_pairs={{0,28},{4,24},{8,20},{12,16},{16,12},{20,8},{24,4},{28,0},{1,29},{... | collective-permute-start | bytes 1474568 | tf_op jit(solution)/shard_map/ppermute | solution.py:800
  289.0 73.5 %collective-permute-start.21 = (bf16[448,128]{1,0:T(8,128)(2,1)}, bf16[448,128]{1,0:T(8,128)(2,1)S(1)}, u32[]{:S(2)}, u32[]{:S(2)}) collective-permute-start(bf16[448,128]{1,0:T(8,128)(2,1)} %get-tuple-element.130), channel_id=1, source_target_pairs={{0,4},{4,0},{8,12},{12,8},{16,20},{20,16},{24,28},{28,24},{1,5},{5... | collective-permute-start | bytes 344072 | tf_op jit(solution)/shard_map/ppermute | solution.py:800
  310.3 52.3 %collective-permute-start.22 = (bf16[448,128]{1,0:T(8,128)(2,1)}, bf16[448,128]{1,0:T(8,128)(2,1)S(1)}, u32[]{:S(2)}, u32[]{:S(2)}) collective-permute-start(bf16[448,128]{1,0:T(8,128)(2,1)} %get-tuple-element.131), channel_id=1, source_target_pairs={{0,8},{4,12},{8,0},{12,4},{16,24},{20,28},{24,16},{28,20},{1,9},{5... | collective-permute-start | bytes 344072 | tf_op jit(solution)/shard_map/ppermute | solution.py:800
  320.9 42.0 %collective-permute-start.23 = (bf16[448,128]{1,0:T(8,128)(2,1)}, bf16[448,128]{1,0:T(8,128)(2,1)S(1)}, u32[]{:S(2)}, u32[]{:S(2)}) collective-permute-start(bf16[448,128]{1,0:T(8,128)(2,1)} %get-tuple-element.132), channel_id=1, source_target_pairs={{0,12},{4,8},{8,4},{12,0},{16,28},{20,24},{24,20},{28,16},{1,13},{... | collective-permute-start | bytes 344072 | tf_op jit(solution)/shard_map/ppermute | solution.py:800
  332.3 33.9 %collective-permute-start.24 = (bf16[448,128]{1,0:T(8,128)(2,1)}, bf16[448,128]{1,0:T(8,128)(2,1)S(1)}, u32[]{:S(2)}, u32[]{:S(2)}) collective-permute-start(bf16[448,128]{1,0:T(8,128)(2,1)} %get-tuple-element.133), channel_id=1, source_target_pairs={{0,16},{4,20},{8,24},{12,28},{16,0},{20,4},{24,8},{28,12},{1,17},{... | collective-permute-start | bytes 344072 | tf_op jit(solution)/shard_map/ppermute | solution.py:800
  362.6 26.4 %collective-permute-start.27 = (bf16[448,128]{1,0:T(8,128)(2,1)S(1)}, bf16[448,128]{1,0:T(8,128)(2,1)S(1)}, u32[]{:S(2)}, u32[]{:S(2)}) collective-permute-start(bf16[448,128]{1,0:T(8,128)(2,1)S(1)} %copy-done.68), channel_id=1, source_target_pairs={{0,28},{4,24},{8,20},{12,16},{16,12},{20,8},{24,4},{28,0},{1,29},{... | collective-permute-start | bytes 344072 | tf_op jit(solution)/shard_map/ppermute | solution.py:800
  362.9 26.2 %collective-permute-start.28 = (bf16[448,128]{1,0:T(8,128)(2,1)}, bf16[448,128]{1,0:T(8,128)(2,1)S(1)}, u32[]{:S(2)}, u32[]{:S(2)}) collective-permute-start(bf16[448,128]{1,0:T(8,128)(2,1)} %get-tuple-element.138), channel_id=1, source_target_pairs={{0,4},{4,0},{8,12},{12,8},{16,20},{20,16},{24,28},{28,24},{1,5},{5... | collective-permute-start | bytes 344072 | tf_op jit(solution)/shard_map/ppermute | solution.py:800
  399.6 25.6 %collective-permute-start.36 = (bf16[448,128]{1,0:T(8,128)(2,1)}, bf16[448,128]{1,0:T(8,128)(2,1)S(1)}, u32[]{:S(2)}, u32[]{:S(2)}) collective-permute-start(bf16[448,128]{1,0:T(8,128)(2,1)} %get-tuple-element.147), channel_id=1, source_target_pairs={{0,8},{4,12},{8,0},{12,4},{16,24},{20,28},{24,16},{28,20},{1,9},{5... | collective-permute-start | bytes 344072 | tf_op jit(solution)/shard_map/ppermute | solution.py:800
  425.2 26.1 %collective-permute-start.41 = (bf16[448,128]{1,0:T(8,128)(2,1)S(1)}, bf16[448,128]{1,0:T(8,128)(2,1)S(1)}, u32[]{:S(2)}, u32[]{:S(2)}) collective-permute-start(bf16[448,128]{1,0:T(8,128)(2,1)S(1)} %copy-done.67), channel_id=1, source_target_pairs={{0,28},{4,24},{8,20},{12,16},{16,12},{20,8},{24,4},{28,0},{1,29},{... | collective-permute-start | bytes 344072 | tf_op jit(solution)/shard_map/ppermute | solution.py:800
  (107 other events, 2576.7 us)
Sparse Core Ops, SparseCore 0:
  10.5 49.4 all-gather.18
  65.7 49.1 all-gather.16
  116.4 48.2 all-gather.14
  166.2 48.3 all-gather.12
  216.5 48.2 all-gather.10
